TPU v7x, 128 devices: a whole 4x4x4 slice. The times are simulated.
128 devices in a mesh: rows: 16 (over y_lo, x, core), snap: 8 (over z, y_hi).
Axes of the slice: x: 4, y: 4 (y_hi: 2, y_lo: 2; y = y_hi * 2 + y_lo), z: 4, core: 2. Of those that a mesh axis runs over, the one named last changes fastest.
Arguments:
- direct: bfloat16 [131072, 1024], P('rows', 'snap'), may hold values from -6 to 6
- adjoint: bfloat16 [131072, 1024], P('rows', 'snap'), may hold values from -6 to 6
- right_vectors: bfloat16 [1024, 256], replicated, may hold values from -0.1875 to 0.1875
- left_vectors: bfloat16 [1024, 256], replicated, may hold values from -0.1875 to 0.1875
- singular: float32 [256], replicated, may hold values from 0.25 to 4
Outputs:
- gram: float32 [1024, 1024], P('snap', 'rows')
- balancing: bfloat16 [131072, 256], P('rows', 'snap')
- adjoint_modes: bfloat16 [131072, 256], P('rows', 'snap')
All inputs are finite; a program needn't handle non-finite values.
Results may differ from a plain program's by a relative error of at most 0.0045.
Values may be sent and summed in bfloat16 or wider, within the bound.
No kernel may reach another device: no remote copies, remote signals or barrier semaphores. Data moves between devices by JAX's collectives and lax.ppermute only.
A program may use at most 128 MiB of HBM per device.

v0:
```python
import jax
import jax.numpy as jnp
from jax import lax
from jax.sharding import PartitionSpec as P


def from_partner(block, axis, bit):
    count = lax.axis_size(axis)
    route = []
    for low in range(count):
        high = low | 1 << bit
        if high != low and high < count:
            route += [(low, high), (high, low)]
    return lax.ppermute(block, axis, route)


def split_up(shard, dim, size):
    lengths = shard.shape
    parts = shard.reshape(*lengths[:dim], size, lengths[dim] // size, *lengths[dim + 1 :])
    return jnp.moveaxis(parts, dim, 0)


def sent_and_summed(shard, axis, dim):
    size = lax.axis_size(axis)
    parts = lax.all_to_all(split_up(shard, dim, size), axis, 0, 0, tiled=True)
    return jnp.sum(parts, axis=0)


def on_device(direct, adjoint, right_vectors, left_vectors, singular):
    local_rows = direct.shape[0]
    block_cols = direct.shape[1]
    modes_all = right_vectors.shape[1]
    nsnap = lax.axis_size("snap")
    mode_cols = modes_all // nsnap
    snap_index = lax.axis_index("snap")
    nrows = local_rows * lax.axis_size("rows")
    mode_start = snap_index * mode_cols
    weights = lax.rsqrt(lax.dynamic_slice_in_dim(singular, mode_start, mode_cols, 0))
    nbits = nsnap.bit_length() - 1
    parity = snap_index % 2
    couple = snap_index // 2
    gathered = direct
    for level in range(1, nbits):
        other = from_partner(gathered, "snap", level)
        upper = snap_index // 2**level % 2
        gathered = jnp.where(
            upper == 1, jnp.concatenate([other, gathered], 1), jnp.concatenate([gathered, other], 1)
        )
    partner_y = from_partner(adjoint, "snap", 0)
    paired = jnp.where(
        parity == 1,
        jnp.concatenate([partner_y, adjoint], 1),
        jnp.concatenate([adjoint, partner_y], 1),
    )
    pair_gram = lax.dot_general(
        paired, gathered, (((0,), (0,)), ((), ())), preferred_element_type=jnp.float32
    )
    lower_rows = pair_gram[:block_cols]
    upper_rows = pair_gram[block_cols:]
    own_rows = jnp.where(parity == 1, upper_rows, lower_rows)
    send_rows = jnp.where(parity == 1, lower_rows, upper_rows)
    recv_rows = from_partner(send_rows.astype(jnp.bfloat16), "snap", 0).astype(send_rows.dtype)
    own_rows = own_rows.reshape(block_cols, nsnap // 2, block_cols)
    recv_rows = recv_rows.reshape(block_cols, nsnap // 2, block_cols)
    even_cols = jnp.where(parity == 0, own_rows, recv_rows)
    odd_cols = jnp.where(parity == 0, recv_rows, own_rows)
    partial_gram = jnp.stack([even_cols, odd_cols], 2).reshape(block_cols, block_cols * nsnap)
    pair_cols = lax.dynamic_slice_in_dim(right_vectors, couple * 2 * mode_cols, 2 * mode_cols, 1)
    pair_cols = pair_cols.reshape(nsnap // 2, 2, block_cols, 2 * mode_cols)
    chosen_v = lax.dynamic_index_in_dim(pair_cols, parity, 1, keepdims=False).reshape(
        -1, 2 * mode_cols
    )
    balance_part = jnp.dot(gathered, chosen_v, preferred_element_type=jnp.float32)
    first_half = balance_part[:, :mode_cols]
    second_half = balance_part[:, mode_cols:]
    own_part = jnp.where(parity == 1, second_half, first_half)
    send_part = jnp.where(parity == 1, first_half, second_half)
    balance_acc = own_part + from_partner(send_part, "snap", 0)
    pair_rows = lax.dynamic_slice_in_dim(left_vectors, couple * 2 * block_cols, 2 * block_cols, 0)
    pair_rows = pair_rows.reshape(2 * block_cols, nsnap // 2, 2, mode_cols)
    chosen_u = lax.dynamic_index_in_dim(pair_rows, parity, 2, keepdims=False).reshape(
        2 * block_cols, -1
    )
    terms = jnp.dot(paired, chosen_u, preferred_element_type=jnp.float32)
    for level in range(nbits - 1, 0, -1):
        half = terms.shape[1] // 2
        low_part = terms[:, :half]
        high_part = terms[:, half:]
        upper = snap_index // 2**level % 2
        keep_part = jnp.where(upper == 1, high_part, low_part)
        give_part = jnp.where(upper == 1, low_part, high_part)
        terms = keep_part + from_partner(give_part, "snap", level)
    gram = sent_and_summed(partial_gram / jnp.sqrt(jnp.float32(nrows)), "rows", 1)
    balancing = (balance_acc * weights).astype(jnp.bfloat16)
    adjoint_modes = (terms * weights).astype(jnp.bfloat16)
    return (gram, balancing, adjoint_modes)


def solution(mesh):
    return jax.shard_map(
        on_device,
        mesh=mesh,
        in_specs=(P("rows", "snap"), P("rows", "snap"), P(), P(), P()),
        out_specs=(P("snap", "rows"), P("rows", "snap"), P("rows", "snap")),
        check_vma=False,
    )
```

profile of v0, /device:TPU:0, one launch (start us, length us, event | category | flops | bytes accessed | tf_op | source)
XLA Modules:
  0.0 258.1 jit_solution(4818328445793682051)
XLA Ops:
  0.6 3.4 %collective-permute-start = (bf16[8192,128]{1,0:T(8,128)(2,1)}, bf16[8192,128]{1,0:T(8,128)(2,1)S(1)}, u32[]{:S(2)}, u32[]{:S(2)}) collective-permute-start(bf16[8192,128]{1,0:T(8,128)(2,1)} %param.6), channel_id=1, source_target_pairs={{0,1},{1,0},{2,3},{3,2},{4,5},{5,4},{6,7},{7,6},{8,9},{9,8},{10,11... | collective-permute-start | bytes 6291464 | tf_op jit(solution)/shard_map/ppermute | solution.py:14
  4.0 1.9 collective-permute-start.1
  6.1 43.8 %collective-permute-done = bf16[8192,128]{1,0:T(8,128)(2,1)S(1)} collective-permute-done((bf16[8192,128]{1,0:T(8,128)(2,1)}, bf16[8192,128]{1,0:T(8,128)(2,1)S(1)}, u32[]{:S(2)}, u32[]{:S(2)}) %collective-permute-start) | collective-permute-done | bytes 2097184 | tf_op jit(solution)/shard_map/ppermute | solution.py:14
  49.9 1.3 copy-done.5
  51.2 3.9 %fusion.2 = f32[8192,128]{0,1:T(8,128)S(1)} fusion(bf16[256,128]{0,1:T(8,128)(2,1)S(1)} %bitcast.17, bf16[8192,128]{1,0:T(8,128)(2,1)} %param.6, bf16[8192,128]{1,0:T(8,128)(2,1)S(1)} %collective-permute-done, pred[]{:T(512)S(6)} %eq.28), kind=kOutput, calls=%fused_computation.11 | convolution fusion | flops 555745280 | bytes 8454145 | tf_op jit(solution)/shard_map/dot_general | solution.py:84
  55.1 2.0 copy-done.1
  57.3 4.0 %collective-permute-start.5 = (f32[8192,64]{0,1:T(8,128)S(1)}, f32[8192,64]{0,1:T(8,128)}, u32[]{:S(2)}, u32[]{:S(2)}) collective-permute-start(f32[8192,64]{0,1:T(8,128)S(1)} %slice_select_fusion), channel_id=1, source_target_pairs={{0,4},{4,0},{1,5},{5,1},{2,6},{6,2},{3,7},{7,3},{8,12},{12,8},{9,1... | collective-permute-start | bytes 6291464 | tf_op jit(solution)/shard_map/ppermute | solution.py:14
  61.3 6.2 %maximum_select_fusion.2 = bf16[8192,256]{1,0:T(8,128)(2,1)} fusion(bf16[8192,128]{1,0:T(8,128)(2,1)} %param.5, bf16[8192,128]{1,0:T(8,128)(2,1)} %collective-permute-done.1, pred[]{:T(512)S(6)} %eq.30), kind=kLoop, calls=%fused_computation.2 | loop fusion | flops 18874368 | bytes 8388609 | tf_op jit(solution)/shard_map/jit(_where)/select_n | solution.py:46
  67.7 40.1 %collective-permute-done.5 = f32[8192,64]{0,1:T(8,128)} collective-permute-done((f32[8192,64]{0,1:T(8,128)S(1)}, f32[8192,64]{0,1:T(8,128)}, u32[]{:S(2)}, u32[]{:S(2)}) %collective-permute-start.5) | collective-permute-done | bytes 2097184 | tf_op jit(solution)/shard_map/ppermute | solution.py:14
  107.9 3.2 %select_add_fusion = f32[8192,64]{0,1:T(8,128)S(1)} fusion(f32[8192,64]{0,1:T(8,128)} %collective-permute-done.5, f32[8192,128]{0,1:T(8,128)} %copy-done.1, pred[]{:T(512)S(6)} %eq.29), kind=kLoop, calls=%fused_computation.3 | loop fusion | flops 1048576 | bytes 8388609 | tf_op jit(solution)/shard_map/add | solution.py:92
  111.0 1.1 slice_select_fusion.1
  112.2 1.6 collective-permute-start.6
  113.7 84.0 %collective-permute-done.2 = bf16[8192,256]{1,0:T(8,128)(2,1)} collective-permute-done((bf16[8192,256]{1,0:T(8,128)(2,1)}, bf16[8192,256]{1,0:T(8,128)(2,1)}, u32[]{:S(2)}, u32[]{:S(2)}) %collective-permute-start.2) | collective-permute-done | bytes 4194336 | tf_op jit(solution)/shard_map/ppermute | solution.py:14
  197.8 8.4 %fusion = f32[8192,64]{0,1:T(8,128)S(1)} fusion(bf16[512,64]{1,0:T(8,128)(2,1)S(1)} %bitcast.16, bf16[8192,256]{1,0:T(8,128)(2,1)} %maximum_select_fusion.2, bf16[8192,256]{1,0:T(8,128)(2,1)} %collective-permute-done.2, pred[]{:T(512)S(6)} %eq.29), kind=kOutput, calls=%fused_computation.5 | convolution fusion | flops 574619648 | bytes 10551297 | tf_op jit(solution)/shard_map/dot_general | solution.py:73
  206.2 1.4 copy-done.2
  207.6 1.1 slice_select_fusion.2
  208.7 3.2 %collective-permute-start.4 = (f32[8192,32]{0,1:T(8,128)}, f32[8192,32]{0,1:T(8,128)}, u32[]{:S(2)}, u32[]{:S(2)}) collective-permute-start(f32[8192,32]{0,1:T(8,128)} %slice_select_fusion.2), channel_id=1, source_target_pairs={{0,1},{1,0},{2,3},{3,2},{4,5},{5,4},{6,7},{7,6},{8,9},{9,8},{10,11... | collective-permute-start | bytes 3145736 | tf_op jit(solution)/shard_map/ppermute | solution.py:14
  211.9 10.0 %fusion.1 = f32[256,512]{1,0:T(8,128)S(1)} fusion(bf16[8192,256]{1,0:T(8,128)(2,1)} %maximum_select_fusion.2, bf16[8192,256]{1,0:T(8,128)(2,1)} %collective-permute-done.2, pred[]{:T(512)S(6)} %eq.29, bf16[8192,128]{1,0:T(8,128)(2,1)S(1)} %copy-done.4, bf16[8192,128]{1,0:T(8,128)(2,1)S(1)} %copy-done.6, pred[]{:T(512)S(6)} %eq.28), kind=kOutput, calls=%fused_computation.6 | convolution fusion | flops 2204106752 | bytes 13107202 | tf_op jit(solution)/shard_map/dot_general | solution.py:55
  222.4 12.6 %collective-permute-done.3 = bf16[128,512]{1,0:T(8,128)(2,1)S(1)} collective-permute-done((bf16[128,512]{1,0:T(8,128)(2,1)S(1)}, bf16[128,512]{1,0:T(8,128)(2,1)S(1)}, u32[]{:S(2)}, u32[]{:S(2)}) %collective-permute-start.3) | collective-permute-done | bytes 131104 | tf_op jit(solution)/shard_map/ppermute | solution.py:14
  235.7 1.1 copy.11
  236.9 0.8 maximum_multiply_fusion
  237.8 5.4 %all-to-all-start = ((f32[16,128,64]{1,2,0:T(8,128)}), f32[16,128,64]{1,2,0:T(8,128)S(1)}, u32[]{:S(2)}, u32[]{:S(2)}) async-start(f32[16,128,64]{1,2,0:T(8,128)} %bitcast.11), calls=%async_computation | async-start | bytes 1048576 | tf_op jit(solution)/shard_map/all_to_all | solution.py:25
  243.3 10.7 %all-to-all-done = f32[16,128,64]{1,2,0:T(8,128)S(1)} async-done(((f32[16,128,64]{1,2,0:T(8,128)}), f32[16,128,64]{1,2,0:T(8,128)S(1)}, u32[]{:S(2)}, u32[]{:S(2)}) %all-to-all-start) | async-done | bytes 524320 | tf_op jit(solution)/shard_map/all_to_all | solution.py:25
  254.7 3.5 %multiply_convert_fusion = (bf16[8192,32]{0,1:T(8,128)(2,1)}, bf16[8192,32]{0,1:T(8,128)(2,1)}) fusion(f32[8192,32]{0,1:T(8,128)} %collective-permute-done.6, f32[8192,64]{0,1:T(8,128)S(1)} %select_add_fusion, f32[32]{0:T(128)S(1)} %dynamic-slice_rsqrt_fusion, pred[]{:T(512)S(6)} %eq.30, f32[8192,32]{0,1:T(8,128)} %collective-permute-done.4, ...), kind=kLoop, calls=%fused_computation.7 | loop fusion | flops 2097152 | bytes 7340162 | tf_op jit(solution)/shard_map/convert_element_type | solution.py:95
  (29 shorter events, 2.6 us)
Async XLA Ops:
  0.6 5.3 %copy-start = (bf16[1024,256]{1,0:T(8,128)(2,1)S(1)}, bf16[1024,256]{1,0:T(8,128)(2,1)}, u32[]{:S(2)}) copy-start(bf16[1024,256]{1,0:T(8,128)(2,1)} %param.8) | copy-start | bytes 1572868
  0.6 49.2 %collective-permute-start = (bf16[8192,128]{1,0:T(8,128)(2,1)}, bf16[8192,128]{1,0:T(8,128)(2,1)S(1)}, u32[]{:S(2)}, u32[]{:S(2)}) collective-permute-start(bf16[8192,128]{1,0:T(8,128)(2,1)} %param.6), channel_id=1, source_target_pairs={{0,1},{1,0},{2,3},{3,2},{4,5},{5,4},{6,7},{7,6},{8,9},{9,8},{10,11... | collective-permute-start | bytes 6291464 | tf_op jit(solution)/shard_map/ppermute | solution.py:14
  4.0 57.3 %collective-permute-start.1 = (bf16[8192,128]{1,0:T(8,128)(2,1)}, bf16[8192,128]{1,0:T(8,128)(2,1)}, u32[]{:S(2)}, u32[]{:S(2)}) collective-permute-start(bf16[8192,128]{1,0:T(8,128)(2,1)} %param.5), channel_id=1, source_target_pairs={{0,2},{2,0},{1,3},{3,1},{4,6},{6,4},{5,7},{7,5},{8,10},{10,8},{9,1... | collective-permute-start | bytes 6291464 | tf_op jit(solution)/shard_map/ppermute | solution.py:14
  49.9 1.3 copy-start.5
  55.1 2.0 copy-start.1
  57.3 50.6 %collective-permute-start.5 = (f32[8192,64]{0,1:T(8,128)S(1)}, f32[8192,64]{0,1:T(8,128)}, u32[]{:S(2)}, u32[]{:S(2)}) collective-permute-start(f32[8192,64]{0,1:T(8,128)S(1)} %slice_select_fusion), channel_id=1, source_target_pairs={{0,4},{4,0},{1,5},{5,1},{2,6},{6,2},{3,7},{7,3},{8,12},{12,8},{9,1... | collective-permute-start | bytes 6291464 | tf_op jit(solution)/shard_map/ppermute | solution.py:14
  61.3 6.3 %copy-start.3 = (bf16[1024,256]{1,0:T(8,128)(2,1)S(1)}, bf16[1024,256]{1,0:T(8,128)(2,1)}, u32[]{:S(2)}) copy-start(bf16[1024,256]{1,0:T(8,128)(2,1)} %param.7) | copy-start | bytes 1572868
  67.5 130.2 %collective-permute-start.2 = (bf16[8192,256]{1,0:T(8,128)(2,1)}, bf16[8192,256]{1,0:T(8,128)(2,1)}, u32[]{:S(2)}, u32[]{:S(2)}) collective-permute-start(bf16[8192,256]{1,0:T(8,128)(2,1)} %maximum_select_fusion.2), channel_id=1, source_target_pairs={{0,4},{4,0},{1,5},{5,1},{2,6},{6,2},{3,7},{7,3},{8,12},{12,8},{9,1... | collective-permute-start | bytes 12582920 | tf_op jit(solution)/shard_map/ppermute | solution.py:14
  112.2 142.5 %collective-permute-start.6 = (f32[8192,32]{0,1:T(8,128)}, f32[8192,32]{0,1:T(8,128)}, u32[]{:S(2)}, u32[]{:S(2)}) collective-permute-start(f32[8192,32]{0,1:T(8,128)} %slice_select_fusion.1), channel_id=1, source_target_pairs={{0,2},{2,0},{1,3},{3,1},{4,6},{6,4},{5,7},{7,5},{8,10},{10,8},{9,1... | collective-permute-start | bytes 3145736 | tf_op jit(solution)/shard_map/ppermute | solution.py:14
  197.7 14.1 %copy-start.4 = (bf16[8192,128]{1,0:T(8,128)(2,1)S(1)}, bf16[8192,128]{1,0:T(8,128)(2,1)}, u32[]{:S(2)}) copy-start(bf16[8192,128]{1,0:T(8,128)(2,1)} %param.6) | copy-start | bytes 6291460
  197.8 14.1 %copy-start.6 = (bf16[8192,128]{1,0:T(8,128)(2,1)S(1)}, bf16[8192,128]{1,0:T(8,128)(2,1)}, u32[]{:S(2)}) copy-start(bf16[8192,128]{1,0:T(8,128)(2,1)} %copy-done.5) | copy-start | bytes 6291460
  206.2 1.4 copy-start.2
  208.7 46.0 %collective-permute-start.4 = (f32[8192,32]{0,1:T(8,128)}, f32[8192,32]{0,1:T(8,128)}, u32[]{:S(2)}, u32[]{:S(2)}) collective-permute-start(f32[8192,32]{0,1:T(8,128)} %slice_select_fusion.2), channel_id=1, source_target_pairs={{0,1},{1,0},{2,3},{3,2},{4,5},{5,4},{6,7},{7,6},{8,9},{9,8},{10,11... | collective-permute-start | bytes 3145736 | tf_op jit(solution)/shard_map/ppermute | solution.py:14
  221.9 21.3 %copy-start.7 = (f32[256]{0:T(256)S(1)}, f32[256]{0:T(256)}, u32[]{:S(2)}) copy-start(f32[256]{0:T(256)} %param.9) | copy-start | bytes 3076
  221.9 13.0 %collective-permute-start.3 = (bf16[128,512]{1,0:T(8,128)(2,1)S(1)}, bf16[128,512]{1,0:T(8,128)(2,1)S(1)}, u32[]{:S(2)}, u32[]{:S(2)}) collective-permute-start(bf16[128,512]{1,0:T(8,128)(2,1)S(1)} %select_convert_fusion), channel_id=1, source_target_pairs={{0,1},{1,0},{2,3},{3,2},{4,5},{5,4},{6,7},{7,6},{8,9},{9,8},{10,11... | collective-permute-start | bytes 393224 | tf_op jit(solution)/shard_map/ppermute | solution.py:14
  237.8 16.3 %all-to-all-start = ((f32[16,128,64]{1,2,0:T(8,128)}), f32[16,128,64]{1,2,0:T(8,128)S(1)}, u32[]{:S(2)}, u32[]{:S(2)}) async-start(f32[16,128,64]{1,2,0:T(8,128)} %bitcast.11), calls=%async_computation | async-start | bytes 1048576 | tf_op jit(solution)/shard_map/all_to_all | solution.py:25
where the time goes:
time: 258 us
  waiting for transfers between devices  191 us (74%)
  matrix products  22.3 us (9%)
  starting transfers between devices  20 us (8%)
  other arithmetic  17.6 us (7%)
  local copies, waits for them, and re-layouts  6.25 us (2%)
    ppermute x7, waiting for transfers between devices, from_partner(): return lax.ppermute(block, axis, route)  181 us
    ppermute x7, starting transfers between devices, from_partner(): return lax.ppermute(block, axis, route)  14.5 us
    all_to_all x1, waiting for transfers between devices, sent_and_summed(): parts = lax.all_to_all(split_up(shard, dim, size), axis, 0, 0, tiled=True)  10.7 us
    dot_general x1, matrix products, on_device(): lax.dot_general(paired, gathered, (((0,), (0,)), ((), ())), preferred_ele...  10 us
    dot_general x1, matrix products, on_device(): jnp.dot(gathered, chosen_v, preferred_element_type=jnp.float32)  8.42 us
    select_n x1, other arithmetic, on_device(): jnp.where(upper == 1, jnp.concatenate([other, gathered], 1), jnp.concaten...  6.22 us
    all_to_all x1, starting transfers between devices, sent_and_summed(): parts = lax.all_to_all(split_up(shard, dim, size), axis, 0, 0, tiled=True)  5.42 us
  transfers between devices with their start and end apart: 8, of which 5 were waited for; matrix products, arithmetic and copies ran while one was open for 15% of the time, Pallas kernels for 0%

commit v1 on v0

v1 whole, which is shorter than its diff:
```python
import jax
import jax.numpy as jnp
from jax import lax
from jax.sharding import PartitionSpec as P


def swap(block, pairs):
    return lax.ppermute(block, ("rows", "snap"), pairs)


def on_device(direct, adjoint, right_vectors, left_vectors, singular):
    nrow, nsnap = lax.axis_size("rows"), lax.axis_size("snap")
    rows, cols = direct.shape
    part = rows // nsnap
    m = cols * nsnap
    r = right_vectors.shape[1]
    width = m // nrow
    bf, f32 = jnp.bfloat16, jnp.float32

    def turned(a):
        return lax.all_to_all(a.reshape(nsnap, part, cols), "snap", 0, 0, tiled=True)

    x8 = turned(direct)
    y8 = turned(adjoint)
    x = x8.transpose(1, 0, 2).reshape(part, m)
    y = y8.transpose(1, 0, 2).reshape(part, m)
    weights = lax.rsqrt(singular)

    def modes(a, v):
        t = lax.dot_general(v, a, (((0,), (1,)), ((), ())), preferred_element_type=f32)
        t = (t * weights[:, None]).astype(bf).reshape(nsnap, r // nsnap, part)
        t = lax.all_to_all(t, "snap", 0, 0, tiled=True)
        return t.transpose(0, 2, 1).reshape(rows, r // nsnap)

    g = lax.dot_general(x, y, (((0,), (0,)), ((), ())), preferred_element_type=f32)
    g = g * (1.0 / jnp.sqrt(f32(rows * nrow)))
    g = g.reshape(2, nrow // 4, 2, width, m)
    ri = lax.axis_index("rows")
    core = ri % 2
    keep = lax.dynamic_index_in_dim(g, core, 2, keepdims=False)
    give = lax.dynamic_index_in_dim(g, 1 - core, 2, keepdims=False).astype(bf)
    pairs = [(i, i ^ 1) for i in range(nrow)]
    g = keep + lax.ppermute(give, "rows", pairs).astype(f32)
    groups = [[yl * (nrow // 2) + xx * 2 + c for xx in range(nrow // 4)] for yl in range(2) for c in range(2)]
    h = g.astype(bf).transpose(1, 0, 2, 3)
    h = lax.all_to_all(h, "rows", 0, 0, axis_index_groups=groups, tiled=True)
    h = jnp.sum(h.astype(f32), axis=0)
    ylo = ri // (nrow // 2)
    keep = lax.dynamic_index_in_dim(h, ylo, 0, keepdims=False)
    give = lax.dynamic_index_in_dim(h, 1 - ylo, 0, keepdims=False).astype(bf)
    pairs = [(i, (i + nrow // 2) % nrow) for i in range(nrow)]
    h = keep + lax.ppermute(give, "rows", pairs).astype(f32)
    h = h.astype(bf).reshape(width, nsnap, cols).transpose(1, 0, 2)
    h = lax.all_to_all(h, "snap", 0, 0, tiled=True)
    gram = jnp.sum(h.astype(f32), axis=0).T
    return gram, modes(x, right_vectors), modes(y, left_vectors)


def solution(mesh):
    return jax.shard_map(
        on_device,
        mesh=mesh,
        in_specs=(P("rows", "snap"), P("rows", "snap"), P(), P(), P()),
        out_specs=(P("snap", "rows"), P("rows", "snap"), P("rows", "snap")),
        check_vma=False,
    )
```

time: 258 us -> 151 us (0.59)
  waiting for transfers between devices: 191 us -> 63.9 us
  blocking collectives: 0 us -> 36.7 us
  matrix products: 22.3 us -> 9.64 us
  other arithmetic: 17.6 us -> 5.38 us
  local copies, waits for them, and re-layouts: 6.25 us -> 12.2 us
    ppermute x7 -> x2, waiting for transfers between devices: 181 us -> 10.6 us  [the longest x1 7.63 us: on_device(): h = keep + lax.ppermute(give, 'rows', pairs).astype(f32)]
    all_to_all x1 -> x5, waiting for transfers between devices: 10.7 us -> 53.3 us  [the longest x1 24.8 us: turned(): lax.all_to_all(a.reshape(nsnap, part, cols), 'snap', 0, 0, tiled=True)]
    all_to_all x0 -> x1, blocking collectives: none -> 36.7 us  [turned(): lax.all_to_all(a.reshape(nsnap, part, cols), 'snap', 0, 0, tiled=True)]
    all_to_all x1 -> x5, starting transfers between devices: 5.42 us -> 21 us  [the longest x2 6.99 us: modes(): t = lax.all_to_all(t, 'snap', 0, 0, tiled=True)]
    ppermute x7 -> x2, starting transfers between devices: 14.5 us -> 0.99 us  [the longest x1 0.99 us: on_device(): h = keep + lax.ppermute(give, 'rows', pairs).astype(f32)]
    dot_general x3, matrix products: 22.3 us -> 9.64 us  [the longest x2 5.68 us: modes(): lax.dot_general(v, a, (((0,), (1,)), ((), ())), preferred_element_type=f32)]
    select_n x5 -> x0, other arithmetic: 9.43 us -> none  [the longest x1 6.22 us: on_device(): jnp.where(upper == 1, jnp.concatenate([other, gathered], 1), jnp.concaten...]
    transpose x0 -> x3, local copies, waits for them, and re-layouts: none -> 7.42 us  [the longest x1 3.89 us: on_device(): y = y8.transpose(1, 0, 2).reshape(part, m)]
  transfers between devices with their start and end apart: 8 -> 7, of which waited for: 5 -> 7; matrix products, arithmetic and copies ran while one was open for 15% -> 8% of each run, Pallas kernels for 0% -> 0%
where the time goes in v1:
time: 151 us
  waiting for transfers between devices  63.9 us (42%)
  blocking collectives  36.7 us (24%)
  starting transfers between devices  21.9 us (15%)
  local copies, waits for them, and re-layouts  12.2 us (8%)
  matrix products  9.64 us (6%)
  other arithmetic  5.38 us (4%)
    all_to_all x1, blocking collectives, turned(): lax.all_to_all(a.reshape(nsnap, part, cols), 'snap', 0, 0, tiled=True)  36.7 us
    all_to_all x1, waiting for transfers between devices, turned(): lax.all_to_all(a.reshape(nsnap, part, cols), 'snap', 0, 0, tiled=True)  24.8 us
    all_to_all x1, waiting for transfers between devices, on_device(): h = lax.all_to_all(h, 'rows', 0, 0, axis_index_groups=groups, tiled=True)  12.6 us
    all_to_all x2, waiting for transfers between devices, modes(): t = lax.all_to_all(t, 'snap', 0, 0, tiled=True)  9.45 us
    ppermute x1, waiting for transfers between devices, on_device(): h = keep + lax.ppermute(give, 'rows', pairs).astype(f32)  7.63 us
    all_to_all x2, starting transfers between devices, modes(): t = lax.all_to_all(t, 'snap', 0, 0, tiled=True)  6.99 us
    all_to_all x1, waiting for transfers between devices, on_device(): h = lax.all_to_all(h, 'snap', 0, 0, tiled=True)  6.54 us
    dot_general x2, matrix products, modes(): lax.dot_general(v, a, (((0,), (1,)), ((), ())), preferred_element_type=f32)  5.68 us
  transfers between devices with their start and end apart: 7, of which 7 were waited for; matrix products, arithmetic and copies ran while one was open for 8% of the time, Pallas kernels for 0%

profile of v1, /device:TPU:0, one launch (start us, length us, event | category | flops | bytes accessed | tf_op | source)
XLA Modules:
  0.0 150.6 jit_solution(3909682756542104862)
XLA Ops:
  0.6 36.7 %all_to_all.30 = bf16[8,1024,128]{2,1,0:T(8,128)(2,1)} all-to-all(bf16[8,1024,128]{2,1,0:T(8,128)(2,1)} %bitcast.52), channel_id=1, replica_groups=mesh['rows'=16,'snap'=8] {'snap'}, dimensions={0} | all-to-all | bytes 4194304 | tf_op jit(solution)/shard_map/all_to_all | solution.py:21
  37.4 4.3 %all-to-all-start.1 = ((bf16[8,1024,128]{2,1,0:T(8,128)(2,1)}), bf16[8,1024,128]{2,1,0:T(8,128)(2,1)}, u32[]{:S(2)}, u32[]{:S(2)}) async-start(bf16[8,1024,128]{2,1,0:T(8,128)(2,1)} %bitcast.3), calls=%async_computation.1 | async-start | bytes 4194304 | tf_op jit(solution)/shard_map/all_to_all | solution.py:21
  41.8 2.9 %copy.22 = bf16[1024,8,128]{0,2,1:T(8,128)(2,1)S(1)} copy(bf16[1024,8,128]{2,0,1:T(8,128)(2,1)} %bitcast.49) | data formatting | bytes 4194304 | tf_op jit(solution)/shard_map/transpose | solution.py:25
  44.6 24.8 %all-to-all-done.1 = bf16[8,1024,128]{2,1,0:T(8,128)(2,1)} async-done(((bf16[8,1024,128]{2,1,0:T(8,128)(2,1)}), bf16[8,1024,128]{2,1,0:T(8,128)(2,1)}, u32[]{:S(2)}, u32[]{:S(2)}) %all-to-all-start.1) | async-done | bytes 2097184 | tf_op jit(solution)/shard_map/all_to_all | solution.py:21
  69.4 3.9 %copy.23 = bf16[1024,8,128]{0,2,1:T(8,128)(2,1)} copy(bf16[1024,8,128]{2,0,1:T(8,128)(2,1)} %bitcast.4) | data formatting | bytes 4194304 | tf_op jit(solution)/shard_map/transpose | solution.py:26
  73.3 4.0 %convolution_multiply_fusion = f32[1024,1024]{1,0:T(8,128)S(1)} fusion(bf16[1024,1024]{0,1:T(8,128)(2,1)S(1)} %bitcast.45, bf16[1024,1024]{0,1:T(8,128)(2,1)} %bitcast.47), kind=kOutput, calls=%fused_computation | convolution fusion | flops 2148532224 | bytes 8388608 | tf_op jit(solution)/shard_map/dot_general | solution.py:35
  77.3 1.9 %copy-done.1 = f32[1024,1024]{1,0:T(8,128)} copy-done((f32[1024,1024]{1,0:T(8,128)}, f32[1024,1024]{1,0:T(8,128)S(1)}, u32[]{:S(2)}) %copy-start.1) | copy-done | bytes 4194328
  79.2 1.1 fusion.4
  80.3 3.0 %collective-permute-done = bf16[2,4,64,1024]{3,2,0,1:T(8,128)(2,1)} collective-permute-done((bf16[2,4,64,1024]{3,2,0,1:T(8,128)(2,1)}, bf16[2,4,64,1024]{3,2,0,1:T(8,128)(2,1)}, u32[]{:S(2)}, u32[]{:S(2)}) %collective-permute-start) | collective-permute-done | bytes 1048608 | tf_op jit(solution)/shard_map/ppermute | solution.py:43
  83.3 3.3 %fusion.3 = bf16[4,2,64,1024]{3,2,1,0:T(8,128)(2,1)} fusion(bf16[2,4,64,1024]{3,2,0,1:T(8,128)(2,1)} %collective-permute-done, f32[2,4,2,64,1024]{4,3,2,1,0:T(8,128)} %bitcast.51, s32[]{:T(128)S(6)} %select_n.26), kind=kLoop, calls=%fused_computation.9 | loop fusion | flops 1572864 | bytes 4194308 | tf_op jit(solution)/shard_map/transpose | solution.py:45
  86.6 4.4 %all-to-all-start.2 = ((bf16[4,2,64,1024]{3,2,1,0:T(8,128)(2,1)}), bf16[4,2,64,1024]{3,2,1,0:T(8,128)(2,1)}, u32[]{:S(2)}, u32[]{:S(2)}) async-start(bf16[4,2,64,1024]{3,2,1,0:T(8,128)(2,1)} %fusion.3), calls=%async_computation.2 | async-start | bytes 2097152 | tf_op jit(solution)/shard_map/all_to_all | solution.py:46
  91.0 3.1 %fusion.2 = bf16[256,1024]{1,0:T(8,128)(2,1)} fusion(bf16[1024,256]{1,0:T(8,128)(2,1)S(1)} %copy-done, bf16[1024,1024]{0,1:T(8,128)(2,1)} %bitcast.48, f32[256]{0:T(256)S(1)} %rsqrt.3), kind=kOutput, calls=%fused_computation.8 | convolution fusion | flops 537395200 | bytes 3146752 | tf_op jit(solution)/shard_map/dot_general | solution.py:30
  94.2 12.6 %all-to-all-done.2 = bf16[4,2,64,1024]{3,2,1,0:T(8,128)(2,1)} async-done(((bf16[4,2,64,1024]{3,2,1,0:T(8,128)(2,1)}), bf16[4,2,64,1024]{3,2,1,0:T(8,128)(2,1)}, u32[]{:S(2)}, u32[]{:S(2)}) %all-to-all-start.2) | async-done | bytes 1048608 | tf_op jit(solution)/shard_map/all_to_all | solution.py:46
  106.7 3.5 %all-to-all-start.5 = ((bf16[8,32,1024]{2,1,0:T(8,128)(2,1)}), bf16[8,32,1024]{2,1,0:T(8,128)(2,1)S(1)}, u32[]{:S(2)}, u32[]{:S(2)}) async-start(bf16[8,32,1024]{2,1,0:T(8,128)(2,1)} %bitcast.56), calls=%async_computation.5 | async-start | bytes 1048576 | tf_op jit(solution)/shard_map/all_to_all | solution.py:32
  110.2 2.6 %fusion.1 = bf16[256,1024]{1,0:T(8,128)(2,1)} fusion(bf16[1024,256]{1,0:T(8,128)(2,1)} %param.7, bf16[1024,1024]{0,1:T(8,128)(2,1)S(1)} %bitcast.46, f32[256]{0:T(256)S(1)} %rsqrt.3), kind=kOutput, calls=%fused_computation.7 | convolution fusion | flops 537395200 | bytes 3146752 | tf_op jit(solution)/shard_map/dot_general | solution.py:30
  112.8 1.5 convert_reduce_fusion
  114.2 7.1 %all-to-all-done.5 = bf16[8,32,1024]{2,1,0:T(8,128)(2,1)S(1)} async-done(((bf16[8,32,1024]{2,1,0:T(8,128)(2,1)}), bf16[8,32,1024]{2,1,0:T(8,128)(2,1)S(1)}, u32[]{:S(2)}, u32[]{:S(2)}) %all-to-all-start.5) | async-done | bytes 524320 | tf_op jit(solution)/shard_map/all_to_all | solution.py:32
  121.4 3.5 %all-to-all-start.4 = ((bf16[8,32,1024]{2,1,0:T(8,128)(2,1)}), bf16[8,32,1024]{2,1,0:T(8,128)(2,1)S(1)}, u32[]{:S(2)}, u32[]{:S(2)}) async-start(bf16[8,32,1024]{2,1,0:T(8,128)(2,1)} %bitcast.55), calls=%async_computation.4 | async-start | bytes 1048576 | tf_op jit(solution)/shard_map/all_to_all | solution.py:32
  124.9 1.0 collective-permute-start.1
  125.9 7.6 %collective-permute-done.1 = bf16[64,1024]{1,0:T(8,128)(2,1)S(1)} collective-permute-done((bf16[64,1024]{1,0:T(8,128)(2,1)S(1)}, bf16[64,1024]{1,0:T(8,128)(2,1)S(1)}, u32[]{:S(2)}, u32[]{:S(2)}) %collective-permute-start.1) | collective-permute-done | bytes 131104 | tf_op jit(solution)/shard_map/ppermute | solution.py:52
  134.3 2.3 %all-to-all-done.4 = bf16[8,32,1024]{2,1,0:T(8,128)(2,1)S(1)} async-done(((bf16[8,32,1024]{2,1,0:T(8,128)(2,1)}), bf16[8,32,1024]{2,1,0:T(8,128)(2,1)S(1)}, u32[]{:S(2)}, u32[]{:S(2)}) %all-to-all-start.4) | async-done | bytes 524320 | tf_op jit(solution)/shard_map/all_to_all | solution.py:32
  136.6 5.2 %all-to-all-start.3 = ((bf16[8,64,128]{2,1,0:T(8,128)(2,1)}), bf16[8,64,128]{2,1,0:T(8,128)(2,1)S(1)}, u32[]{:S(2)}, u32[]{:S(2)}) async-start(bf16[8,64,128]{2,1,0:T(8,128)(2,1)} %copy.26), calls=%async_computation.3 | async-start | bytes 262144 | tf_op jit(solution)/shard_map/all_to_all | solution.py:54
  141.8 0.8 copy.31
  143.4 6.5 %all-to-all-done.3 = bf16[8,64,128]{2,1,0:T(8,128)(2,1)S(1)} async-done(((bf16[8,64,128]{2,1,0:T(8,128)(2,1)}), bf16[8,64,128]{2,1,0:T(8,128)(2,1)S(1)}, u32[]{:S(2)}, u32[]{:S(2)}) %all-to-all-start.3) | async-done | bytes 131104 | tf_op jit(solution)/shard_map/all_to_all | solution.py:54
  (13 shorter events, 2.2 us)
Async XLA Ops:
  0.6 90.4 %copy-start = (bf16[1024,256]{1,0:T(8,128)(2,1)S(1)}, bf16[1024,256]{1,0:T(8,128)(2,1)}, u32[]{:S(2)}) copy-start(bf16[1024,256]{1,0:T(8,128)(2,1)} %param.8) | copy-start | bytes 1572868
  37.4 32.0 %all-to-all-start.1 = ((bf16[8,1024,128]{2,1,0:T(8,128)(2,1)}), bf16[8,1024,128]{2,1,0:T(8,128)(2,1)}, u32[]{:S(2)}, u32[]{:S(2)}) async-start(bf16[8,1024,128]{2,1,0:T(8,128)(2,1)} %bitcast.3), calls=%async_computation.1 | async-start | bytes 4194304 | tf_op jit(solution)/shard_map/all_to_all | solution.py:21
  77.2 1.9 %copy-start.1 = (f32[1024,1024]{1,0:T(8,128)}, f32[1024,1024]{1,0:T(8,128)S(1)}, u32[]{:S(2)}) copy-start(f32[1024,1024]{1,0:T(8,128)S(1)} %convolution_multiply_fusion) | copy-start | bytes 12582916
  80.3 3.0 %collective-permute-start = (bf16[2,4,64,1024]{3,2,0,1:T(8,128)(2,1)}, bf16[2,4,64,1024]{3,2,0,1:T(8,128)(2,1)}, u32[]{:S(2)}, u32[]{:S(2)}) collective-permute-start(bf16[2,4,64,1024]{3,2,0,1:T(8,128)(2,1)} %fusion.4), channel_id=1, source_target_pairs={{0,8},{8,0},{16,24},{24,16},{32,40},{40,32},{48,56},{56,48},{64,72... | collective-permute-start | bytes 3145736 | tf_op jit(solution)/shard_map/ppermute | solution.py:43
  86.6 4.4 %copy-start.2 = (f32[256]{0:T(256)S(1)}, f32[256]{0:T(256)}, u32[]{:S(2)}) copy-start(f32[256]{0:T(256)} %param.9) | copy-start | bytes 3076
  86.6 20.1 %all-to-all-start.2 = ((bf16[4,2,64,1024]{3,2,1,0:T(8,128)(2,1)}), bf16[4,2,64,1024]{3,2,1,0:T(8,128)(2,1)}, u32[]{:S(2)}, u32[]{:S(2)}) async-start(bf16[4,2,64,1024]{3,2,1,0:T(8,128)(2,1)} %fusion.3), calls=%async_computation.2 | async-start | bytes 2097152 | tf_op jit(solution)/shard_map/all_to_all | solution.py:46
  106.7 14.7 %all-to-all-start.5 = ((bf16[8,32,1024]{2,1,0:T(8,128)(2,1)}), bf16[8,32,1024]{2,1,0:T(8,128)(2,1)S(1)}, u32[]{:S(2)}, u32[]{:S(2)}) async-start(bf16[8,32,1024]{2,1,0:T(8,128)(2,1)} %bitcast.56), calls=%async_computation.5 | async-start | bytes 1048576 | tf_op jit(solution)/shard_map/all_to_all | solution.py:32
  121.4 15.2 %all-to-all-start.4 = ((bf16[8,32,1024]{2,1,0:T(8,128)(2,1)}), bf16[8,32,1024]{2,1,0:T(8,128)(2,1)S(1)}, u32[]{:S(2)}, u32[]{:S(2)}) async-start(bf16[8,32,1024]{2,1,0:T(8,128)(2,1)} %bitcast.55), calls=%async_computation.4 | async-start | bytes 1048576 | tf_op jit(solution)/shard_map/all_to_all | solution.py:32
  124.9 8.6 %collective-permute-start.1 = (bf16[64,1024]{1,0:T(8,128)(2,1)S(1)}, bf16[64,1024]{1,0:T(8,128)(2,1)S(1)}, u32[]{:S(2)}, u32[]{:S(2)}) collective-permute-start(bf16[64,1024]{1,0:T(8,128)(2,1)S(1)} %fusion.6), channel_id=1, source_target_pairs={{0,64},{8,72},{16,80},{24,88},{32,96},{40,104},{48,112},{56,120},{... | collective-permute-start | bytes 393224 | tf_op jit(solution)/shard_map/ppermute | solution.py:52
  136.6 13.4 %all-to-all-start.3 = ((bf16[8,64,128]{2,1,0:T(8,128)(2,1)}), bf16[8,64,128]{2,1,0:T(8,128)(2,1)S(1)}, u32[]{:S(2)}, u32[]{:S(2)}) async-start(bf16[8,64,128]{2,1,0:T(8,128)(2,1)} %copy.26), calls=%async_computation.3 | async-start | bytes 262144 | tf_op jit(solution)/shard_map/all_to_all | solution.py:54
